TPU v7x, 32 devices: a whole 2x2x4 slice. The times are simulated.
32 devices in a mesh: replica: 8 (over z, y), expert: 4 (over x, core).
Axes of the slice: x: 2, y: 2, z: 4, core: 2. Of those that a mesh axis runs over, the one named last changes fastest.
Arguments:
- local_params: bfloat16 [8, 128, 48, 2048], P('replica', 'expert'), may hold values from -13 to 13, as said below
- base: bfloat16 [128, 48, 2048], P('expert'), may hold values from -6 to 6, as said below
- momentum: float32 [128, 48, 2048], P('expert', None, 'replica'), may hold values from -1.5 to 1.5
- touched: int32 [8, 128], P('replica', 'expert'), may hold values from 0 to 1, as said below
- counts: int32 [8, 128], P('replica', 'expert'), may hold values from 32 to 352, as said below
Outputs:
- new_params: bfloat16 [8, 128, 48, 2048], P('replica', 'expert')
- new_momentum: float32 [128, 48, 2048], P('expert', None, 'replica')
Inputs may be any that keep to these rules, and one draw needn't show every extreme that they name: `touched`: among the 32 experts on one device along the `expert` axis, each replica touches at most 16; in every such group some replica touches exactly 16. Positive token counts. `local_params`: Real-valued weights. `base`: Real-valued weights.
All inputs are finite; a program needn't handle non-finite values. Where the computation divides by a largest or mean magnitude, that divisor is 1e-20 or more.
Results may differ from a plain program's by a relative error of at most 0.0045.
Values may be sent and summed in bfloat16 or wider, within the bound.
No kernel may reach another device: no remote copies, remote signals or barrier semaphores. Data moves between devices by JAX's collectives and lax.ppermute only.
A program may use at most 128 MiB of HBM per device.

v0:
```python
import jax
import jax.numpy as jnp
from jax import lax
from jax.sharding import PartitionSpec as P

BLOCK = 128
CAP = 16


EPSILON = 1e-06
CLIP_RATIO = 0.02
NESTEROV = 0.9
OUTER_LR = 0.7


def encode(difference):
    leading = difference.shape[:-1]
    blocks = difference.reshape(leading + (difference.shape[-1] // BLOCK, BLOCK))
    block_scale = (jnp.max(jnp.abs(blocks), axis=-1) + EPSILON).astype(jnp.bfloat16)
    code_vals = (blocks / block_scale.astype(jnp.float32)[..., None]).astype(jnp.bfloat16)
    return (code_vals.reshape(difference.shape), block_scale)


def decode(code_vals, block_scale):
    leading = code_vals.shape[:-1]
    blocks = code_vals.astype(jnp.float32).reshape(leading + (block_scale.shape[-1], -1))
    return (blocks * block_scale.astype(jnp.float32)[..., None]).reshape(code_vals.shape)


def slot_onehot(flag_rows):
    ranking = jnp.cumsum(flag_rows, axis=-1) - 1
    slot_range = jnp.arange(CAP, dtype=jnp.int32)
    return (flag_rows[..., None, :] == 1) & (ranking[..., None, :] == slot_range[:, None])


def slot_indices(onehot):
    expert_range = jnp.arange(onehot.shape[-1], dtype=jnp.int32)
    return jnp.sum(onehot.astype(jnp.int32) * expert_range, axis=-1)


def local(local_params, base, momentum, touched, counts):
    replicas = lax.axis_size("replica")
    local_experts = base.shape[0]
    all_touched, all_counts = (
        lax.all_gather(touched, "replica", axis=0, tiled=True),
        lax.all_gather(counts, "replica", axis=0, tiled=True),
    )
    weights = (all_touched * all_counts).astype(jnp.float32)
    weight_sum = jnp.maximum(jnp.sum(weights, axis=0), 1.0)
    base_wide = base.astype(jnp.float32)
    code_vals, block_scale = encode(base_wide - local_params[0].astype(jnp.float32))
    all_onehot = slot_onehot(all_touched)
    own_slots = slot_indices(slot_onehot(touched[0]))
    packed = (jnp.take(code_vals, own_slots, axis=0), jnp.take(block_scale, own_slots, axis=0))
    got_codes, got_scale = (
        lax.all_to_all(packed[0], "replica", split_axis=2, concat_axis=0, tiled=True),
        lax.all_to_all(packed[1], "replica", split_axis=2, concat_axis=0, tiled=True),
    )
    pieces = decode(got_codes, got_scale).reshape((replicas, CAP) + got_codes.shape[1:])
    mixing = all_onehot.astype(jnp.float32) * weights[:, None, :]
    weighted = jnp.einsum("sjx,sjrc->xrc", mixing, pieces, precision=lax.Precision.HIGHEST)
    pseudo = weighted / weight_sum[:, None, None]
    whole_square = lax.psum(jnp.sum(pseudo * pseudo), ("replica", "expert"))
    entries = local_experts * lax.axis_size("expert") * base.shape[1] * base.shape[2]
    factor = jnp.minimum(1.0, CLIP_RATIO / jnp.sqrt(whole_square / entries + EPSILON))
    clipped = factor * pseudo
    new_momentum = NESTEROV * momentum + clipped
    outer_step = -OUTER_LR * (clipped + NESTEROV * new_momentum)
    step_code, step_scale = encode(outer_step)
    full_codes, full_scale = (
        lax.all_gather(step_code, "replica", axis=2, tiled=True),
        lax.all_gather(step_scale, "replica", axis=2, tiled=True),
    )
    updated = base_wide + decode(full_codes, full_scale)
    renewed = updated.astype(jnp.bfloat16)
    new_params = jnp.where(touched[0][:, None, None] == 1, renewed, local_params[0])[None]
    return (new_params, new_momentum)


def solution(mesh):
    return jax.shard_map(
        local,
        mesh=mesh,
        in_specs=(
            P("replica", "expert", None, None),
            P("expert", None, None),
            P("expert", None, "replica"),
            P("replica", "expert"),
            P("replica", "expert"),
        ),
        out_specs=(P("replica", "expert", None, None), P("expert", None, "replica")),
        check_vma=False,
    )
```

profile of v0, /device:TPU:0, one launch (start us, length us, event | category | flops | bytes accessed | tf_op | source)
XLA Modules:
  0.0 482.5 jit_solution(17457529464907678122)
XLA Ops:
  7.2 0.7 compare_bitcast_fusion
  7.8 0.7 copy.91
  8.6 0.1 reduce-window.8
  8.6 0.1 add_reduce_fusion
  8.7 0.1 select_reduce_fusion
  8.9 17.3 %fusion.1 = f32[32,48,2048]{2,0,1:T(8,128)} fusion(bf16[1,32,48,2048]{3,2,1,0:T(8,128)(2,1)} %param.5, bf16[32,48,2048]{2,1,0:T(8,128)(2,1)} %param.6), kind=kLoop, calls=%fused_computation.6 | loop fusion | flops 12582912 | bytes 25165824 | tf_op jit(solution)/shard_map/abs | solution.py:19
  26.1 12.1 %copy.108 = f32[192,8,16,128]{3,2,1,0:T(8,128)} copy(f32[192,8,16,128]{3,1,2,0:T(8,128)} %bitcast.66) | data formatting | bytes 25165824
  38.3 19.1 %reduce_max.18 = f32[32,48,16]{2,0,1:T(8,128)S(1)} reduce(f32[32,48,16,128]{3,2,0,1:T(8,128)} %bitcast.65, f32[]{:T(128)} %constant.36.clone.1), dimensions={3}, to_apply=%region_3.4 | reduce | flops 3121152 | bytes 12681220 | tf_op jit(solution)/shard_map/reduce_max | solution.py:19
  57.4 0.4 copy.93
  57.9 0.6 gather_fusion.1
  58.5 0.1 broadcast_select_fusion.1
  58.6 0.7 reshape.134
  59.3 7.3 %all-to-all-start.1 = ((bf16[8,2,768]{2,1,0:T(2,128)(2,1)}), bf16[8,2,768]{2,1,0:T(2,128)(2,1)S(1)}, u32[]{:S(2)}, u32[]{:S(2)}) async-start(bf16[8,2,768]{2,1,0:T(2,128)(2,1)} %reshape.134), calls=%async_computation.1 | async-start | bytes 49152 | tf_op jit(solution)/shard_map/all_to_all | solution.py:57
  66.6 0.6 copy.94
  67.3 7.1 %div.36 = f32[32,48,16,128]{3,2,0,1:T(8,128)} broadcast(f32[32,48,16]{2,0,1:T(8,128)S(1)} %copy.94), dimensions={0,1,2} | broadcast | bytes 12681216 | tf_op jit(solution)/shard_map/div | solution.py:20
  74.4 13.6 %div.37 = f32[32,48,2048]{2,0,1:T(8,128)} reshape(f32[32,48,16,128]{3,2,0,1:T(8,128)} %div.36) | data formatting | bytes 25165824 | tf_op jit(solution)/shard_map/div | solution.py:20
  88.0 13.8 %divide_convert_fusion = bf16[32,48,2048]{2,0,1:T(8,128)(2,1)S(1)} fusion(f32[32,48,2048]{2,0,1:T(8,128)} %div.37, bf16[1,32,48,2048]{3,2,1,0:T(8,128)(2,1)} %param.5, bf16[32,48,2048]{2,1,0:T(8,128)(2,1)} %param.6), kind=kLoop, calls=%fused_computation.5 | loop fusion | flops 15728640 | bytes 31457280 | tf_op jit(solution)/shard_map/convert_element_type | solution.py:20
  101.8 6.2 %copy.95 = bf16[32,48,2048]{2,1,0:T(8,128)(2,1)} copy(bf16[32,48,2048]{2,0,1:T(8,128)(2,1)S(1)} %divide_convert_fusion) | data formatting | bytes 12582912 | tf_op jit(solution)/shard_map/convert_element_type | solution.py:20
  108.0 3.5 gather_fusion
  111.5 2.0 broadcast_select_fusion
  113.6 10.5 %copy.96 = bf16[16,48,2048]{1,0,2:T(8,128)(2,1)} copy(bf16[16,48,2048]{2,1,0:T(8,128)(2,1)} %broadcast_select_fusion) | data formatting | bytes 6291456 | tf_op jit(solution)/shard_map/jit(_take)/select_n | solution.py:54
  124.0 0.0 copy-start.2
  124.0 0.0 copy-start.3
  124.0 14.3 %reshape.136 = bf16[8,2,98304]{2,1,0:T(2,128)(2,1)} reshape(bf16[2048,16,48]{2,1,0:T(8,128)(2,1)} %bitcast.68) | data formatting | bytes 6291456
  138.3 0.0 all-to-all-done.1
  138.3 6.0 %all-to-all-start = ((bf16[8,2,98304]{2,1,0:T(2,128)(2,1)}), bf16[8,2,98304]{2,1,0:T(2,128)(2,1)S(1)}, u32[]{:S(2)}, u32[]{:S(2)}) async-start(bf16[8,2,98304]{2,1,0:T(2,128)(2,1)} %reshape.136), calls=%async_computation | async-start | bytes 6291456 | tf_op jit(solution)/shard_map/all_to_all | solution.py:56
  144.3 0.0 all-gather.4.cloned.1.call-start
  144.4 0.0 copy-done.2
  144.4 65.6 %all-gather = s32[8,1,32]{2,1,0:T(1,128)S(1)} all-gather(s32[1,1,32]{2,1,0:T(1,128)S(1)} %bitcast.77), channel_id=1, replica_groups=mesh['replica'=8,'expert'=4] {'replica'}, dimensions={0}, use_global_device_ids=true | all-gather | bytes 1152 | tf_op jit(solution)/shard_map/all_gather | solution.py:45
  209.9 0.2 reduce_window_sum.18
  210.1 0.0 copy-done.3
  210.1 31.5 %all-gather.1 = s32[8,1,32]{2,1,0:T(1,128)S(1)} all-gather(s32[1,1,32]{2,1,0:T(1,128)S(1)} %bitcast.78), channel_id=1, replica_groups=mesh['replica'=8,'expert'=4] {'replica'}, dimensions={0}, use_global_device_ids=true | all-gather | bytes 1152 | tf_op jit(solution)/shard_map/all_gather | solution.py:46
  241.7 0.1 reshape.135
  241.8 3.6 copy.100
  245.4 9.2 %mul.67 = f32[128,48,2,128]{3,2,0,1:T(2,128)} broadcast(f32[128,48,2]{2,0,1:T(8,128)} %copy.100), dimensions={0,1,2} | broadcast | bytes 6340608 | tf_op jit(solution)/shard_map/mul | solution.py:27
  254.6 8.9 %mul.68 = f32[8,16,48,256]{3,1,0,2:T(8,128)} reshape(f32[128,48,2,128]{3,2,0,1:T(2,128)} %mul.67) | data formatting | bytes 12582912 | tf_op jit(solution)/shard_map/mul | solution.py:27
  263.6 0.0 all-to-all-done
  263.6 9.3 %reshape.137 = bf16[2048,16,48]{2,1,0:T(8,128)(2,1)} reshape(bf16[8,2,98304]{2,1,0:T(2,128)(2,1)S(1)} %all-to-all-done) | data formatting | bytes 6291456
  272.9 13.1 %copy.97 = f32[16,48,8,256]{3,0,2,1:T(8,128)} copy(bf16[16,48,8,256]{1,0,3,2:T(8,128)(2,1)} %bitcast.67) | data formatting | bytes 9437184 | tf_op jit(solution)/shard_map/convert_element_type | solution.py:26
  286.0 0.0 copy-start.1
  286.0 7.4 %multiply_reduce_fusion = (f32[]{:T(128)}, f32[32,48,256]{2,0,1:T(8,128)S(1)}) fusion(f32[32]{0:T(128)S(1)} %broadcast_maximum_fusion, f32[8,16,48,256]{3,1,0,2:T(8,128)} %mul.68, f32[16,48,8,256]{3,0,2,1:T(8,128)} %copy.97, f32[8,32]{1,0:T(8,128)S(1)} %get-tuple-element.17, s32[8,32]{1,0:T(8,128)S(1)} %broadcast_add_fusion, ...), kind=kOutput, calls=%fused_computation.17 | convolution fusion | flops 606744576 | bytes 14158212 | tf_op jit(solution)/shard_map/sjx,sjrc->xrc/dot_general | solution.py:61
  293.3 37.4 %psum.7 = f32[]{:T(128)} all-reduce(f32[]{:T(128)} %get-tuple-element.20), channel_id=1, replica_groups=mesh['replica'=8,'expert'=4] {'replica','expert'}, use_global_device_ids=true, to_apply=%region_6.7 | all-reduce | flops 1 | bytes 8 | tf_op jit(solution)/shard_map/psum | solution.py:63
  331.4 0.0 copy-done.1
  331.5 2.9 fusion.5
  334.4 2.1 abs.15
  336.5 2.6 reduce_max.19
  339.0 1.6 copy.102
  340.6 1.5 copy.103
  342.1 3.3 div.43
  345.5 2.4 div.44
  347.9 3.9 divide_convert_fusion.1
  351.8 0.0 all-gather.4.cloned.1.call-update
  351.8 32.0 %all_gather.15 = bf16[32,48,16]{1,0,2:T(8,128)(2,1)S(1)} all-gather(bf16[32,48,2]{1,0,2:T(8,128)(2,1)S(1)} %add_convert_fusion.1), channel_id=1, replica_groups=mesh['replica'=8,'expert'=4] {'replica'}, dimensions={2}, use_global_device_ids=true | all-gather | bytes 55296 | tf_op jit(solution)/shard_map/all_gather | solution.py:72
  383.8 0.6 copy.104
  384.5 7.1 %mul.77 = f32[32,48,16,128]{3,2,0,1:T(8,128)} broadcast(f32[32,48,16]{2,0,1:T(8,128)S(1)} %copy.104), dimensions={0,1,2} | broadcast | bytes 12681216 | tf_op jit(solution)/shard_map/mul | solution.py:27
  391.6 0.0 copy-start
  391.6 13.8 %mul.78 = f32[32,48,2048]{2,0,1:T(8,128)} reshape(f32[32,48,16,128]{3,2,0,1:T(8,128)} %mul.77) | data formatting | bytes 25165824 | tf_op jit(solution)/shard_map/mul | solution.py:27
  405.4 0.0 copy-done
  405.4 2.1 copy.106
  407.4 46.7 %all-gather.4.cloned.1.call-done = bf16[32,48,2048]{2,0,1:T(8,128)(2,1)} async-done(((bf16[32,48,256]{2,0,1:T(8,128)(2,1)}), bf16[32,48,2048]{2,0,1:T(8,128)(2,1)}) %all-gather.4.cloned.1.call-update) | async-done | bytes 6291472 | tf_op jit(solution)/shard_map/all_gather | solution.py:71
  454.2 15.2 %fusion.3 = bf16[1,32,48,2048]{3,1,2,0:T(8,128)(2,1)S(1)} fusion(f32[32,48,2048]{2,0,1:T(8,128)} %mul.78, bf16[32,48,2048]{2,0,1:T(8,128)(2,1)} %all-gather.4.cloned.1.call-done, pred[32]{0:T(512)(128)(4,1)S(1)} %compare_bitcast_fusion, bf16[1,32,48,2048]{3,2,1,0:T(8,128)(2,1)} %param.5, bf16[32,48,2048]{2,1,0:T(8,128)(2,1)} %param.6), kind=kLoop, calls=%fused_computation.8 | loop fusion | flops 18874368 | bytes 37748768 | tf_op jit(solution)/shard_map/broadcast_in_dim | solution.py:76
  469.3 6.2 %copy.105 = bf16[1,32,48,2048]{3,2,1,0:T(8,128)(2,1)} copy(bf16[1,32,48,2048]{3,1,2,0:T(8,128)(2,1)S(1)} %fusion.3) | data formatting | bytes 12582912
  (12 shorter events, 0.1 us)
Async XLA Ops:
  59.3 79.0 %all-to-all-start.1 = ((bf16[8,2,768]{2,1,0:T(2,128)(2,1)}), bf16[8,2,768]{2,1,0:T(2,128)(2,1)S(1)}, u32[]{:S(2)}, u32[]{:S(2)}) async-start(bf16[8,2,768]{2,1,0:T(2,128)(2,1)} %reshape.134), calls=%async_computation.1 | async-start | bytes 49152 | tf_op jit(solution)/shard_map/all_to_all | solution.py:57
  124.0 20.3 %copy-start.2 = (s32[1,32]{1,0:T(1,128)S(1)}, s32[1,32]{1,0:T(1,128)}, u32[]{:S(2)}) copy-start(s32[1,32]{1,0:T(1,128)} %param.8) | copy-start | bytes 388
  124.0 86.1 %copy-start.3 = (s32[1,32]{1,0:T(1,128)S(1)}, s32[1,32]{1,0:T(1,128)}, u32[]{:S(2)}) copy-start(s32[1,32]{1,0:T(1,128)} %param.9) | copy-start | bytes 388
  138.3 125.2 %all-to-all-start = ((bf16[8,2,98304]{2,1,0:T(2,128)(2,1)}), bf16[8,2,98304]{2,1,0:T(2,128)(2,1)S(1)}, u32[]{:S(2)}, u32[]{:S(2)}) async-start(bf16[8,2,98304]{2,1,0:T(2,128)(2,1)} %reshape.136), calls=%async_computation | async-start | bytes 6291456 | tf_op jit(solution)/shard_map/all_to_all | solution.py:56
  144.3 309.8 %all-gather.4.cloned.1.call-start = ((), (), s32[]{:S(2)}) async-start(), calls=%async_computation.2 | async-start | bytes 7077888 | tf_op jit(solution)/shard_map/all_gather | solution.py:71
  286.0 45.5 %copy-start.1 = (f32[32,48,256]{2,1,0:T(8,128)S(1)}, f32[32,48,256]{2,1,0:T(8,128)}, u32[]{:S(2)}) copy-start(f32[32,48,256]{2,1,0:T(8,128)} %param.7) | copy-start | bytes 4718596
  391.6 13.8 %copy-start = (f32[32,48,256]{2,0,1:T(8,128)S(1)}, f32[32,48,256]{2,0,1:T(8,128)}, u32[]{:S(2)}) copy-start(f32[32,48,256]{2,0,1:T(8,128)} %get-tuple-element.18) | copy-start | bytes 4718596
Sparse Core Ops, SparseCore 0:
  352.0 102.1 all-gather.3
where the time goes:
time: 487 us; the launch traced here: 483 us
  blocking collectives  166 us (34%)
  local copies, waits for them, and re-layouts  155 us (32%)
  other arithmetic  78.2 us (16%)
  waiting for transfers between devices  46.7 us (10%)
  between operations  15.1 us (3%)
  starting transfers between devices  13.3 us (3%)
  matrix products  7.36 us (2%)
    all_gather x1, blocking collectives, local(): lax.all_gather(touched, 'replica', axis=0, tiled=True)  65.6 us
    all_gather x1, waiting for transfers between devices, local(): lax.all_gather(step_code, 'replica', axis=2, tiled=True)  46.7 us
    unnamed x15, local copies, waits for them, and re-layouts  44.8 us
    mul x4, local copies, waits for them, and re-layouts, decode(): blocks * block_scale.astype(jnp.float32)[..., None]  39 us
    psum x1, blocking collectives, local(): whole_square = lax.psum(jnp.sum(pseudo * pseudo), ('replica', 'expert'))  37.4 us
    all_gather x1, blocking collectives, local(): lax.all_gather(step_scale, 'replica', axis=2, tiled=True)  32 us
    all_gather x1, blocking collectives, local(): lax.all_gather(counts, 'replica', axis=0, tiled=True)  31.5 us
    div x4, local copies, waits for them, and re-layouts, encode(): blocks / block_scale.astype(jnp.float32)[..., None]  26.5 us
  transfers between devices with their start and end apart: 3, of which 1 were waited for; matrix products, arithmetic and copies ran while one was open for 24% of the time, Pallas kernels for 0%

commit v1 on v0

v1 whole, which is shorter than its diff:
```python
import functools

import jax
import jax.numpy as jnp
from jax import lax
from jax.experimental import pallas as pl
from jax.experimental.pallas import tpu as pltpu
from jax.sharding import PartitionSpec as P

CAP = 16
EPSILON = 1e-06
CLIP_RATIO = 0.02
NESTEROV = 0.9
OUTER_LR = 0.7


def slot_table(flags):
    experts = flags.shape[-1]
    e = jnp.arange(experts, dtype=jnp.int32)
    before = (e[:, None] < e[None, :]).astype(jnp.int32)
    rank = jnp.sum(flags[..., :, None] * before, axis=-2)
    slot = jnp.arange(CAP, dtype=jnp.int32)
    hit = (flags[..., None, :] == 1) & (rank[..., None, :] == slot[:, None])
    return jnp.sum(jnp.where(hit, e, 0), axis=-1), rank, jnp.sum(flags, axis=-1)


def butterfly(x, axis, size):
    d = 1
    while d < size:
        x = x + lax.ppermute(x, axis, [(i, i ^ d) for i in range(size)])
        d *= 2
    return x


def pack_kernel(slots, weight, base, params, out, *, owners):
    j = pl.program_id(0)
    w = weight[j].astype(jnp.float32)
    diff = (base[0].astype(jnp.float32) - params[0].astype(jnp.float32)) * w
    wide = diff.shape[1] // owners
    for o in range(owners):
        out[o, 0] = diff[:, o * wide:(o + 1) * wide].astype(jnp.bfloat16)


def reduce_kernel(slot, weight, got, pseudo, square, *, replicas, experts):
    def body(e, acc):
        total = jnp.zeros(pseudo.shape[1:], jnp.float32)
        wsum = jnp.float32(0)
        for r in range(replicas):
            w = weight[r, e].astype(jnp.float32)
            wsum += w
            piece = got[r, jnp.minimum(slot[r, e], CAP - 1)].astype(jnp.float32)
            total += jnp.where(w > 0, piece, 0.0)
        total = total / jnp.full((1, 1), jnp.maximum(wsum, 1.0))
        pseudo[e] = total
        return acc + total * total

    acc = lax.fori_loop(0, experts, body, jnp.zeros(pseudo.shape[1:], jnp.float32))
    square[...] = _fold(acc)


def _fold(acc):
    out = jnp.zeros((8, 128), jnp.float32)
    for i in range(acc.shape[0] // 8):
        for k in range(acc.shape[1] // 128):
            out += acc[i * 8:(i + 1) * 8, k * 128:(k + 1) * 128]
    return out


def step_kernel(slots, square, pseudo, momentum, new_momentum, packed, steps, *, replicas, experts, entries):
    total = jnp.sum(jnp.sum(square[...], axis=0, keepdims=True), axis=1, keepdims=True)
    factor = jnp.minimum(1.0, CLIP_RATIO / jnp.sqrt(total / entries + EPSILON))

    def body(e, _):
        clipped = factor * pseudo[e]
        renewed = NESTEROV * momentum[e] + clipped
        new_momentum[e] = renewed
        steps[e] = (-OUTER_LR * (clipped + NESTEROV * renewed)).astype(jnp.bfloat16)
        return 0

    lax.fori_loop(0, experts, body, 0)

    def fill(j, _):
        for r in range(replicas):
            packed[r, j] = steps[slots[r, j]]
        return 0

    lax.fori_loop(0, CAP, fill, 0)


def keep_kernel(flag, params, out, hold, sem_in, sem_out, *, experts):
    def each(fn):
        def body(e, _):
            pl.when(flag[e] == 0)(lambda: fn(e))
            return 0

        lax.fori_loop(0, experts, body, 0)

    def copy_in(e):
        return pltpu.make_async_copy(params.at[e], hold.at[e], sem_in.at[e])

    def copy_out(e):
        return pltpu.make_async_copy(hold.at[e], out.at[e], sem_out.at[e])

    def turn(e):
        copy_in(e).wait()
        copy_out(e).start()

    each(lambda e: copy_in(e).start())
    each(turn)
    each(lambda e: copy_out(e).wait())


def apply_kernel(slots, count, base, params, step, kept, out, *, owners):
    j = pl.program_id(0)
    wide = base.shape[2] // owners

    @pl.when((j == 0) & (count[0] == 0))
    def _():
        out[0] = params[0]

    @pl.when(j < count[0])
    def _():
        for o in range(owners):
            cols = slice(o * wide, (o + 1) * wide)
            out[0, :, cols] = (base[0, :, cols].astype(jnp.float32) + step[o, 0].astype(jnp.float32)).astype(jnp.bfloat16)


def local(local_params, base, momentum, touched, counts):
    replicas = lax.axis_size("replica")
    shards = lax.axis_size("expert")
    experts, rows, width = base.shape
    wide = width // replicas
    params = local_params[0]
    f32, bf16, i32 = jnp.float32, jnp.bfloat16, jnp.int32
    smem = pl.BlockSpec(memory_space=pltpu.SMEM)
    vmem = pl.BlockSpec(memory_space=pltpu.VMEM)
    hbm = pl.BlockSpec(memory_space=pl.ANY)

    own = lax.axis_index("replica")
    mine = jnp.stack([touched[0], touched[0] * counts[0]])
    place = (jnp.arange(replicas, dtype=i32) == own).astype(i32)
    meta = butterfly(place[:, None, None] * mine, "replica", replicas)

    own_slots, _, own_count = slot_table(touched[0])
    live = jnp.arange(CAP, dtype=i32) < own_count
    last = jnp.max(jnp.where(live, own_slots, 0))
    own_slots = jnp.where(live, own_slots, last)
    own_weight = jnp.where(live, jnp.take(counts[0], own_slots), 0)

    packed = pl.pallas_call(
        functools.partial(pack_kernel, owners=replicas),
        grid_spec=pltpu.PrefetchScalarGridSpec(
            num_scalar_prefetch=2,
            grid=(CAP,),
            in_specs=[pl.BlockSpec((1, rows, width), lambda j, s, w: (s[j], 0, 0))] * 2,
            out_specs=pl.BlockSpec((replicas, 1, rows, wide), lambda j, s, w: (0, j, 0, 0)),
        ),
        out_shape=jax.ShapeDtypeStruct((replicas, CAP, rows, wide), bf16),
        name="pack",
    )(own_slots, own_weight, base, params)

    got = lax.all_to_all(packed, "replica", split_axis=0, concat_axis=0, tiled=True)

    all_slots, all_rank, _ = slot_table(meta[:, 0])
    pseudo, square = pl.pallas_call(
        functools.partial(reduce_kernel, replicas=replicas, experts=experts),
        in_specs=[smem, smem, vmem],
        out_specs=[vmem, vmem],
        out_shape=[jax.ShapeDtypeStruct((experts, rows, wide), f32), jax.ShapeDtypeStruct((8, 128), f32)],
        name="reduce",
    )(all_rank, meta[:, 1], got)

    square = butterfly(butterfly(square, "expert", shards), "replica", replicas)

    new_momentum, packed = pl.pallas_call(
        functools.partial(step_kernel, replicas=replicas, experts=experts, entries=experts * shards * rows * width),
        in_specs=[smem, vmem, vmem, vmem],
        out_specs=[vmem, vmem],
        out_shape=[jax.ShapeDtypeStruct((experts, rows, wide), f32), jax.ShapeDtypeStruct((replicas, CAP, rows, wide), bf16)],
        scratch_shapes=[pltpu.VMEM((experts, rows, wide), bf16)],
        name="step",
    )(all_slots, square, pseudo, momentum)

    got = lax.all_to_all(packed, "replica", split_axis=0, concat_axis=0, tiled=True)

    kept = pl.pallas_call(
        functools.partial(keep_kernel, experts=experts),
        in_specs=[smem, hbm],
        out_specs=hbm,
        out_shape=jax.ShapeDtypeStruct(params.shape, bf16),
        scratch_shapes=[pltpu.VMEM(params.shape, bf16), pltpu.SemaphoreType.DMA((experts,)), pltpu.SemaphoreType.DMA((experts,))],
        name="keep",
    )(touched[0], params)

    new_params = pl.pallas_call(
        functools.partial(apply_kernel, owners=replicas),
        grid_spec=pltpu.PrefetchScalarGridSpec(
            num_scalar_prefetch=2,
            grid=(CAP,),
            in_specs=[
                pl.BlockSpec((1, rows, width), lambda j, s, c: (s[j], 0, 0)),
                pl.BlockSpec((1, rows, width), lambda j, s, c: (s[0], 0, 0)),
                pl.BlockSpec((replicas, 1, rows, wide), lambda j, s, c: (0, j, 0, 0)),
                hbm,
            ],
            out_specs=pl.BlockSpec((1, rows, width), lambda j, s, c: (s[j], 0, 0)),
        ),
        out_shape=jax.ShapeDtypeStruct(params.shape, bf16),
        input_output_aliases={5: 0},
        name="apply",
    )(own_slots, own_count[None], base, params, got, kept)
    return new_params[None], new_momentum


def solution(mesh):
    return jax.shard_map(
        local,
        mesh=mesh,
        in_specs=(
            P("replica", "expert", None, None),
            P("expert", None, None),
            P("expert", None, "replica"),
            P("replica", "expert"),
            P("replica", "expert"),
        ),
        out_specs=(P("replica", "expert", None, None), P("expert", None, "replica")),
        check_vma=False,
    )
```

time: 487 us -> 214 us (0.44)
  blocking collectives: 166 us -> 0 us
  local copies, waits for them, and re-layouts: 155 us -> 5.23 us
  waiting for transfers between devices: 46.7 us -> 140 us
  other arithmetic: 78.2 us -> 10.2 us
  Pallas kernels: 0 us -> 37.7 us
  between operations: 15.1 us -> 0.7 us
  matrix products: 7.36 us -> 0 us
  starting transfers between devices: 13.3 us -> 19.7 us
    all_gather x3 -> x0, blocking collectives: 129 us -> none  [the longest x1 65.6 us: local(): lax.all_gather(touched, 'replica', axis=0, tiled=True)]
    ppermute x0 -> x8, waiting for transfers between devices: none -> 77.2 us  [butterfly(): x = x + lax.ppermute(x, axis, [(i, i ^ d) for i in range(size)])]
    all_to_all x2, waiting for transfers between devices: 0.01 us -> 62.7 us  [local(): lax.all_to_all(packed, 'replica', split_axis=0, concat_axis=0, tiled=True)]
    all_gather x1 -> x0, waiting for transfers between devices: 46.7 us -> none  [local(): lax.all_gather(step_code, 'replica', axis=2, tiled=True)]
    unnamed x15 -> x8, local copies, waits for them, and re-layouts: 44.8 us -> 3.32 us
    mul x4 -> x0, local copies, waits for them, and re-layouts: 39 us -> none  [decode(): blocks * block_scale.astype(jnp.float32)[..., None]]
    pallas_call x0 -> x5, Pallas kernels: none -> 37.7 us  [the longest x1 12.2 us: local(): pl.pallas_call(functools.partial(apply_kernel, owners=replicas), grid_spe...]
    psum x1 -> x0, blocking collectives: 37.4 us -> none  [local(): whole_square = lax.psum(jnp.sum(pseudo * pseudo), ('replica', 'expert'))]
  transfers between devices with their start and end apart: 3 -> 10, of which waited for: 1 -> 9; matrix products, arithmetic and copies ran while one was open for 24% -> 1% of each run, Pallas kernels for 0% -> 2%
where the time goes in v1:
time: 214 us; the launch traced here: 213 us
  waiting for transfers between devices  140 us (65%)
  Pallas kernels  37.7 us (18%)
  starting transfers between devices  19.7 us (9%)
  other arithmetic  10.2 us (5%)
  local copies, waits for them, and re-layouts  5.23 us (2%)
    ppermute x8, waiting for transfers between devices, butterfly(): x = x + lax.ppermute(x, axis, [(i, i ^ d) for i in range(size)])  77.2 us
    all_to_all x2, waiting for transfers between devices, local(): lax.all_to_all(packed, 'replica', split_axis=0, concat_axis=0, tiled=True)  62.7 us
    pallas_call x1, Pallas kernels, local(): pl.pallas_call(functools.partial(apply_kernel, owners=replicas), grid_spe...  12.2 us
    pallas_call x1, Pallas kernels, local(): pl.pallas_call(functools.partial(pack_kernel, owners=replicas), grid_spec...  11.5 us
    ppermute x8, starting transfers between devices, butterfly(): x = x + lax.ppermute(x, axis, [(i, i ^ d) for i in range(size)])  9.99 us
    all_to_all x2, starting transfers between devices, local(): lax.all_to_all(packed, 'replica', split_axis=0, concat_axis=0, tiled=True)  9.68 us
    pallas_call x1, Pallas kernels, local(): pl.pallas_call(functools.partial(step_kernel, replicas=replicas, experts=...  4.97 us
    pallas_call x1, Pallas kernels, local(): pl.pallas_call(functools.partial(reduce_kernel, replicas=replicas, expert...  4.91 us
  transfers between devices with their start and end apart: 10, of which 9 were waited for; matrix products, arithmetic and copies ran while one was open for 1% of the time, Pallas kernels for 2%

profile of v1, /device:TPU:0, one launch (start us, length us, event | category | flops | bytes accessed | tf_op | source)
XLA Modules:
  0.0 213.4 jit_solution(8367411680180791942)
XLA Ops:
  0.6 0.7 compare_bitcast_fusion.1
  1.3 0.7 select_reduce_fusion.1
  2.0 1.3 fusion.8
  3.4 0.1 select_reduce_fusion.2
  3.5 1.3 select_reduce_fusion.3
  4.7 1.3 fusion.5
  6.0 1.3 gather_fusion
  7.3 1.8 fusion.4
  9.2 11.5 %pack.1 = bf16[8,16,48,256]{3,2,1,0:T(8,128)(2,1)} custom-call(s32[16]{0:T(128)} %get-tuple-element.11.slots, s32[16]{0:T(128)} %get-tuple-element.10.weight, bf16[32,48,2048]{2,1,0:T(8,128)(2,1)} %base.3, bf16[32,48,2048]{2,1,0:T(8,128)(2,1)} %bitcast.20), custom_call_target="tpu_custom_call" | custom-call | tf_op jit(solution)/shard_map/pack/pallas_call | solution.py:150
  20.7 0.0 copy-start.3
  20.7 6.0 %all-to-all-start = ((bf16[8,16,48,256]{3,2,1,0:T(8,128)(2,1)}), bf16[8,16,48,256]{3,2,1,0:T(8,128)(2,1)S(1)}, u32[]{:S(2)}, u32[]{:S(2)}) async-start(bf16[8,16,48,256]{3,2,1,0:T(8,128)(2,1)} %pack.1), calls=%async_computation | async-start | bytes 6291456 | tf_op jit(solution)/shard_map/all_to_all | solution.py:162
  26.7 0.0 copy-done.3
  26.7 0.1 broadcast_multiply_fusion
  26.8 2.0 collective-permute-start
  28.8 24.0 %collective-permute-done = s32[8,2,32]{2,0,1:T(8,128)S(1)} collective-permute-done((s32[8,2,32]{2,0,1:T(8,128)S(1)}, s32[8,2,32]{2,0,1:T(8,128)S(1)}, u32[]{:S(2)}, u32[]{:S(2)}) %collective-permute-start) | collective-permute-done | bytes 2080 | tf_op jit(solution)/shard_map/ppermute | solution.py:30
  52.8 0.1 fusion.3
  52.9 1.7 collective-permute-start.1
  54.6 24.8 %collective-permute-done.1 = s32[8,2,32]{2,0,1:T(8,128)S(1)} collective-permute-done((s32[8,2,32]{2,0,1:T(8,128)S(1)}, s32[8,2,32]{2,0,1:T(8,128)S(1)}, u32[]{:S(2)}, u32[]{:S(2)}) %collective-permute-start.1) | collective-permute-done | bytes 2080 | tf_op jit(solution)/shard_map/ppermute | solution.py:30
  79.4 0.1 fusion.9
  79.5 3.4 %collective-permute-start.2 = (s32[8,2,32]{2,0,1:T(8,128)S(1)}, s32[8,2,32]{2,0,1:T(8,128)S(1)}, u32[]{:S(2)}, u32[]{:S(2)}) collective-permute-start(s32[8,2,32]{2,0,1:T(8,128)S(1)} %fusion.9), channel_id=1, source_target_pairs={{0,16},{4,20},{8,24},{12,28},{16,0},{20,4},{24,8},{28,12},{1,17},{... | collective-permute-start | bytes 6152 | tf_op jit(solution)/shard_map/ppermute | solution.py:30
  82.8 15.4 %collective-permute-done.2 = s32[8,2,32]{2,0,1:T(8,128)S(1)} collective-permute-done((s32[8,2,32]{2,0,1:T(8,128)S(1)}, s32[8,2,32]{2,0,1:T(8,128)S(1)}, u32[]{:S(2)}, u32[]{:S(2)}) %collective-permute-start.2) | collective-permute-done | bytes 2080 | tf_op jit(solution)/shard_map/ppermute | solution.py:30
  98.2 0.6 slice_bitcast_fusion
  98.8 0.7 multiply_reduce_fusion.slot
  99.5 0.0 copy-start.2
  99.5 0.0 all-to-all-done.got
  99.5 0.0 copy-start
  99.5 1.7 copy-done
  101.2 4.9 %reduce.2 = (f32[32,48,256]{2,1,0:T(8,128)}, f32[8,128]{1,0:T(8,128)}) custom-call(s32[8,32]{1,0:T(8,128)} %multiply_reduce_fusion.slot, s32[8,32]{1,0:T(8,128)} %get-tuple-element.12.weight, bf16[8,16,48,256]{3,2,1,0:T(8,128)(2,1)} %copy-done), custom_call_target="tpu_custom_call" | custom-call | tf_op jit(solution)/shard_map/reduce/pallas_call | solution.py:165
  106.1 0.0 collective-permute-start.3
  106.1 1.4 collective-permute-done.3
  107.5 0.7 add.44
  108.2 0.6 collective-permute-start.4
  108.7 3.0 %collective-permute-done.4 = f32[8,128]{1,0:T(8,128)S(1)} collective-permute-done((f32[8,128]{1,0:T(8,128)S(1)}, f32[8,128]{1,0:T(8,128)S(1)}, u32[]{:S(2)}, u32[]{:S(2)}) %collective-permute-start.4) | collective-permute-done | bytes 4128 | tf_op jit(solution)/shard_map/ppermute | solution.py:30
  111.8 1.5 collective-permute-start.5
  113.2 2.1 %collective-permute-done.5 = f32[8,128]{1,0:T(8,128)S(1)} collective-permute-done((f32[8,128]{1,0:T(8,128)S(1)}, f32[8,128]{1,0:T(8,128)S(1)}, u32[]{:S(2)}, u32[]{:S(2)}) %collective-permute-start.5) | collective-permute-done | bytes 4128 | tf_op jit(solution)/shard_map/ppermute | solution.py:30
  115.4 0.0 collective-permute-start.6
  115.4 3.6 %collective-permute-done.6 = f32[8,128]{1,0:T(8,128)S(1)} collective-permute-done((f32[8,128]{1,0:T(8,128)S(1)}, f32[8,128]{1,0:T(8,128)S(1)}, u32[]{:S(2)}, u32[]{:S(2)}) %collective-permute-start.6) | collective-permute-done | bytes 4128 | tf_op jit(solution)/shard_map/ppermute | solution.py:30
  119.0 0.8 collective-permute-start.7
  119.8 0.0 copy-done.2
  119.8 0.8 select_reduce_fusion.slots
  120.6 2.9 %collective-permute-done.7 = f32[8,128]{1,0:T(8,128)S(1)} collective-permute-done((f32[8,128]{1,0:T(8,128)S(1)}, f32[8,128]{1,0:T(8,128)S(1)}, u32[]{:S(2)}, u32[]{:S(2)}) %collective-permute-start.7) | collective-permute-done | bytes 4128 | tf_op jit(solution)/shard_map/ppermute | solution.py:30
  123.5 0.6 add.48.square
  124.1 5.0 %step.1 = (f32[32,48,256]{2,1,0:T(8,128)}, bf16[8,16,48,256]{3,2,1,0:T(8,128)(2,1)}) custom-call(s32[8,16]{1,0:T(8,128)} %select_reduce_fusion.slots, f32[8,128]{1,0:T(8,128)} %add.48.square, f32[32,48,256]{2,1,0:T(8,128)} %get-tuple-element.7.pseudo, f32[32,48,256]{2,1,0:T(8,128)} %momentum.1), custom_call_target="tpu_custom_call" | custom-call | tf_op jit(solution)/shard_map/step/pallas_call | solution.py:175
  129.1 3.6 %all-to-all-start.1 = ((bf16[8,16,48,256]{3,2,1,0:T(8,128)(2,1)}), bf16[8,16,48,256]{3,2,1,0:T(8,128)(2,1)S(1)}, u32[]{:S(2)}, u32[]{:S(2)}) async-start(bf16[8,16,48,256]{3,2,1,0:T(8,128)(2,1)} %get-tuple-element.8), calls=%async_computation.1 | async-start | bytes 6291456 | tf_op jit(solution)/shard_map/all_to_all | solution.py:184
  132.7 4.2 %keep.1.kept = bf16[32,48,2048]{2,1,0:T(8,128)(2,1)} custom-call(s32[32]{0:T(128)} %bitcast.25, bf16[32,48,2048]{2,1,0:T(8,128)(2,1)} %bitcast.21), custom_call_target="tpu_custom_call" | custom-call | tf_op jit(solution)/shard_map/keep/pallas_call | solution.py:186
  136.9 62.7 %all-to-all-done.1.step = bf16[8,16,48,256]{3,2,1,0:T(8,128)(2,1)S(1)} async-done(((bf16[8,16,48,256]{3,2,1,0:T(8,128)(2,1)}), bf16[8,16,48,256]{3,2,1,0:T(8,128)(2,1)S(1)}, u32[]{:S(2)}, u32[]{:S(2)}) %all-to-all-start.1) | async-done | bytes 3145760 | tf_op jit(solution)/shard_map/all_to_all | solution.py:184
  199.6 0.0 copy-start.1
  199.6 1.6 copy-done.1
  201.2 12.2 %apply.1 = bf16[32,48,2048]{2,1,0:T(8,128)(2,1)} custom-call(s32[16]{0:T(128)} %get-tuple-element.11.slots, s32[1]{0:T(128)} %bitcast.2.count, bf16[32,48,2048]{2,1,0:T(8,128)(2,1)} %base.3, bf16[32,48,2048]{2,1,0:T(8,128)(2,1)} %bitcast.22, bf16[8,16,48,256]{3,2,1,0:T(8,128)(2,1)} %copy-done.1, ...), custom_call_target="tpu_custom_call", output_to_operand_aliasing={{}: (5, {})} | custom-call | tf_op jit(solution)/shard_map/apply/pallas_call | solution.py:195
  (9 shorter events, 0.0 us)
Async XLA Ops:
  20.7 6.0 %copy-start.3 = (s32[1,32]{1,0:T(1,128)S(1)}, s32[1,32]{1,0:T(1,128)}, u32[]{:S(2)}) copy-start(s32[1,32]{1,0:T(1,128)} %param.8) | copy-start | bytes 388
  20.7 78.9 %all-to-all-start = ((bf16[8,16,48,256]{3,2,1,0:T(8,128)(2,1)}), bf16[8,16,48,256]{3,2,1,0:T(8,128)(2,1)S(1)}, u32[]{:S(2)}, u32[]{:S(2)}) async-start(bf16[8,16,48,256]{3,2,1,0:T(8,128)(2,1)} %pack.1), calls=%async_computation | async-start | bytes 6291456 | tf_op jit(solution)/shard_map/all_to_all | solution.py:162
  26.8 26.0 %collective-permute-start = (s32[8,2,32]{2,0,1:T(8,128)S(1)}, s32[8,2,32]{2,0,1:T(8,128)S(1)}, u32[]{:S(2)}, u32[]{:S(2)}) collective-permute-start(s32[8,2,32]{2,0,1:T(8,128)S(1)} %broadcast_multiply_fusion), channel_id=1, source_target_pairs={{0,4},{4,0},{8,12},{12,8},{16,20},{20,16},{24,28},{28,24},{1,5},{5... | collective-permute-start | bytes 6152 | tf_op jit(solution)/shard_map/ppermute | solution.py:30
  52.9 26.5 %collective-permute-start.1 = (s32[8,2,32]{2,0,1:T(8,128)S(1)}, s32[8,2,32]{2,0,1:T(8,128)S(1)}, u32[]{:S(2)}, u32[]{:S(2)}) collective-permute-start(s32[8,2,32]{2,0,1:T(8,128)S(1)} %fusion.3), channel_id=1, source_target_pairs={{0,8},{4,12},{8,0},{12,4},{16,24},{20,28},{24,16},{28,20},{1,9},{5... | collective-permute-start | bytes 6152 | tf_op jit(solution)/shard_map/ppermute | solution.py:30
  79.5 18.8 %collective-permute-start.2 = (s32[8,2,32]{2,0,1:T(8,128)S(1)}, s32[8,2,32]{2,0,1:T(8,128)S(1)}, u32[]{:S(2)}, u32[]{:S(2)}) collective-permute-start(s32[8,2,32]{2,0,1:T(8,128)S(1)} %fusion.9), channel_id=1, source_target_pairs={{0,16},{4,20},{8,24},{12,28},{16,0},{20,4},{24,8},{28,12},{1,17},{... | collective-permute-start | bytes 6152 | tf_op jit(solution)/shard_map/ppermute | solution.py:30
  99.5 20.3 %copy-start.2 = (s32[8,32]{1,0:T(8,128)S(1)}, s32[8,32]{1,0:T(8,128)}, u32[]{:S(2)}) copy-start(s32[8,32]{1,0:T(8,128)} %multiply_reduce_fusion.slot) | copy-start | bytes 3076
  99.5 1.7 copy-start
  106.1 1.4 collective-permute-start.3
  108.2 3.6 %collective-permute-start.4 = (f32[8,128]{1,0:T(8,128)S(1)}, f32[8,128]{1,0:T(8,128)S(1)}, u32[]{:S(2)}, u32[]{:S(2)}) collective-permute-start(f32[8,128]{1,0:T(8,128)S(1)} %add.44), channel_id=1, source_target_pairs={{0,2},{1,3},{2,0},{3,1},{4,6},{5,7},{6,4},{7,5},{8,10},{9,11},{10,... | collective-permute-start | bytes 12296 | tf_op jit(solution)/shard_map/ppermute | solution.py:30
  111.8 3.6 %collective-permute-start.5 = (f32[8,128]{1,0:T(8,128)S(1)}, f32[8,128]{1,0:T(8,128)S(1)}, u32[]{:S(2)}, u32[]{:S(2)}) collective-permute-start(f32[8,128]{1,0:T(8,128)S(1)} %add.45), channel_id=1, source_target_pairs={{0,4},{4,0},{8,12},{12,8},{16,20},{20,16},{24,28},{28,24},{1,5},{5... | collective-permute-start | bytes 12296 | tf_op jit(solution)/shard_map/ppermute | solution.py:30
  115.4 3.6 %collective-permute-start.6 = (f32[8,128]{1,0:T(8,128)S(1)}, f32[8,128]{1,0:T(8,128)S(1)}, u32[]{:S(2)}, u32[]{:S(2)}) collective-permute-start(f32[8,128]{1,0:T(8,128)S(1)} %add.46), channel_id=1, source_target_pairs={{0,8},{4,12},{8,0},{12,4},{16,24},{20,28},{24,16},{28,20},{1,9},{5... | collective-permute-start | bytes 12296 | tf_op jit(solution)/shard_map/ppermute | solution.py:30
  119.0 4.5 %collective-permute-start.7 = (f32[8,128]{1,0:T(8,128)S(1)}, f32[8,128]{1,0:T(8,128)S(1)}, u32[]{:S(2)}, u32[]{:S(2)}) collective-permute-start(f32[8,128]{1,0:T(8,128)S(1)} %add.47), channel_id=1, source_target_pairs={{0,16},{4,20},{8,24},{12,28},{16,0},{20,4},{24,8},{28,12},{1,17},{... | collective-permute-start | bytes 12296 | tf_op jit(solution)/shard_map/ppermute | solution.py:30
  129.1 70.5 %all-to-all-start.1 = ((bf16[8,16,48,256]{3,2,1,0:T(8,128)(2,1)}), bf16[8,16,48,256]{3,2,1,0:T(8,128)(2,1)S(1)}, u32[]{:S(2)}, u32[]{:S(2)}) async-start(bf16[8,16,48,256]{3,2,1,0:T(8,128)(2,1)} %get-tuple-element.8), calls=%async_computation.1 | async-start | bytes 6291456 | tf_op jit(solution)/shard_map/all_to_all | solution.py:184
  199.6 1.6 copy-start.1
